TPU v7x, 256 devices: a whole 4x4x8 slice. The times are simulated.
256 devices in a mesh: section: 8 (over x, z_lo), dp: 32 (over y, z_hi, core).
Axes of the slice: x: 4, y: 4, z: 8 (z_hi: 4, z_lo: 2; z = z_hi * 2 + z_lo), core: 2. Of those that a mesh axis runs over, the one named last changes fastest.
Arguments:
- activations: bfloat16 [64, 512, 4608], P('section', 'dp'), may hold values from -6 to 6
- section_sources: int32 [64], replicated, may hold values from 0 to 63, as said below
- accumulators: float32 [1024, 16, 4608], P('dp', 'section'), may hold values from -6 to 6
- block_sources: int32 [1024], replicated, may hold values from 0 to 1023, as said below
- loss_terms: float32 [8, 32], P('section', 'dp'), may hold values from 0.35 to 6
- pre_gain: float32 [8, 4608], P('section'), may hold values from 0.1 to 1.9
- query_weight: bfloat16 [8, 4608, 4096], P('section', None, 'dp'), may hold values from -0.09375 to 0.09375
- keyval_weight: bfloat16 [8, 4608, 4096], P('section', None, 'dp'), may hold values from -0.09375 to 0.09375
- output_weight: bfloat16 [8, 4096, 4608], P('section', 'dp'), may hold values from -0.09375 to 0.09375
- post_gain: float32 [8, 4608], P('section'), may hold values from 0.1 to 1.9
Outputs:
- new_activations: bfloat16 [64, 512, 4608], P('section', 'dp')
- new_accumulators: float32 [1024, 16, 4608], P('dp', 'section')
- check_out: bfloat16 [8, 512, 4608], P('section', 'dp')
Inputs may be any that keep to these rules, and one draw needn't show every extreme that they name: `section_sources`: A permutation; each old section's micro-batches fill 1 slots of each new section. `block_sources`: A permutation; each old data index's blocks fill 1 block of each new data index.
All inputs are finite; a program needn't handle non-finite values.
Results may differ from a plain program's by a relative error of at most 0.014.
Values may be sent and summed in bfloat16 or wider, within the bound.
A program may use at most 64 MiB of HBM per device.

v0:
```python
import jax
import jax.numpy as jnp
from jax import lax
from jax.sharding import PartitionSpec as P

D = 4608


def sent_together(arrays, axis, split_dim, concat_dim, along):
    columns = [a.reshape(*a.shape[:along], -1) for a in arrays]
    both = jnp.concatenate(columns, axis=along)
    result, at, finished = (
        lax.all_to_all(both, axis, split_axis=split_dim, concat_axis=concat_dim, tiled=True),
        0,
        [],
    )
    for a, column in zip(arrays, columns):
        piece = result[..., at : at + column.shape[along]]
        finished.append(piece.reshape(*piece.shape[:along], *a.shape[along:]))
        at += column.shape[along]
    return tuple(finished)


def partner(value, axis, stride):
    mask = 2**stride
    pairs = [(source, source ^ mask) for source in range(lax.axis_size(axis))]
    return lax.ppermute(value, axis, pairs)


def rms_norm(values, gain):
    meansq = jnp.mean(values * values, axis=-1, keepdims=True)
    return values * lax.rsqrt(meansq + 1e-06) * gain


def rotary(values, positions):
    width = values.shape[-1]
    middle = width // 2
    counter = jnp.arange(middle, dtype=jnp.float32)
    freqs = 10000.0 ** (-2.0 * counter / width)
    angles = positions.astype(jnp.float32)[:, None] * freqs[None, :]
    cosine = jnp.cos(angles)
    sine = jnp.sin(angles)
    first = values[..., :middle]
    second = values[..., middle:]
    return jnp.concatenate(
        [first * cosine - second * sine, second * cosine + first * sine], axis=-1
    )


def plan_routes(sources, own_index, groups, per_group):
    per_peer = per_group // groups
    table = sources.reshape(groups, per_group)
    owners = table // per_group
    places = table % per_group
    slot_ids = jnp.arange(per_group, dtype=jnp.int32)
    sort_keys = jnp.where(owners == own_index, slot_ids[None, :], slot_ids[None, :] + per_group)
    ranking = jnp.argsort(sort_keys, axis=1)[:, :per_peer]
    send_index = jnp.take_along_axis(places, ranking, axis=1).reshape(-1)
    my_owners = lax.dynamic_slice_in_dim(owners, own_index, 1, 0)[0]
    earlier = (my_owners[None, :] == my_owners[:, None]) & (slot_ids[None, :] < slot_ids[:, None])
    earlier_count = jnp.sum(earlier.astype(jnp.int32), axis=1)
    recv_index = my_owners * per_peer + earlier_count
    return (send_index, recv_index)


def on_device(
    activations,
    section_sources,
    accumulators,
    block_sources,
    loss_terms,
    pre_gain,
    query_weight,
    keyval_weight,
    output_weight,
    post_gain,
):
    sections = lax.axis_size("section")
    section_index = lax.axis_index("section")
    mb_local = activations.shape[0]
    send_index, recv_index = plan_routes(section_sources, section_index, sections, mb_local)
    outgoing = jnp.take(activations, send_index, axis=0)
    incoming = lax.all_to_all(outgoing, "section", split_axis=0, concat_axis=0, tiled=True)
    moved = jnp.take(incoming, recv_index, axis=0)
    data_ranks = lax.axis_size("dp")
    data_index = lax.axis_index("dp")
    blk_local = accumulators.shape[0]
    per_peer = blk_local // data_ranks
    block_send, block_recv = plan_routes(block_sources, data_index, data_ranks, blk_local)
    outgoing_blocks = jnp.take(accumulators, block_send, axis=0)
    term_rows = jnp.broadcast_to(loss_terms, (blk_local, 1))
    incoming_blocks, incoming_terms = tuple(
        (
            part.astype(jnp.float32)
            for part in sent_together(
                (outgoing_blocks.astype(jnp.bfloat16), term_rows.astype(jnp.bfloat16)),
                "dp",
                0,
                0,
                1,
            )
        )
    )
    scale_sum = jnp.sum(incoming_terms[::per_peer, 0])
    factor = data_ranks / scale_sum
    new_accumulators = jnp.take(incoming_blocks, block_recv, axis=0) * factor
    checked = moved[0]
    head_size = query_weight.shape[2]
    is_even = data_index % 2 == 0
    w_query = query_weight[0]
    w_keyval = keyval_weight[0]
    gain_pre = pre_gain[0]
    block_rows = lax.all_gather(checked, "dp", axis=0, tiled=True)
    row_count = block_rows.shape[0]
    positions = jnp.arange(row_count, dtype=jnp.int32)
    normed = rms_norm(block_rows.astype(jnp.float32), gain_pre).astype(jnp.bfloat16)
    queries = jnp.dot(normed, w_query, preferred_element_type=jnp.float32)
    own_proj = jnp.dot(normed, w_keyval, preferred_element_type=jnp.float32)
    queries = rotary(queries, positions)
    own_proj = jnp.where(is_even, rotary(own_proj, positions), own_proj)
    projected = jnp.concatenate([queries, own_proj], axis=1).astype(jnp.bfloat16)
    queries = projected[:, :head_size]
    own_kv = projected[:, head_size:]
    partner_kv = partner(own_kv, "dp", 0)
    key_rows = jnp.where(is_even, own_kv, partner_kv)
    value_rows = jnp.where(is_even, partner_kv, own_kv)
    length = projected.shape[0]
    positions = jnp.arange(length, dtype=jnp.int32)
    scale_factor = (D / data_ranks) ** (-0.5)
    scores = (
        lax.dot_general(
            queries, key_rows, (((1,), (1,)), ((), ())), preferred_element_type=jnp.float32
        )
        * scale_factor
    )
    capped = 50.0 * jnp.tanh(scores / 50.0)
    causal = positions[None, :] <= positions[:, None]
    expd = jnp.where(causal, jnp.exp(capped), 0.0)
    denominator = jnp.sum(expd, axis=-1, keepdims=True)
    probs = expd.astype(jnp.bfloat16)
    numer = jnp.dot(probs, value_rows, preferred_element_type=jnp.float32)
    attended = (numer / denominator).astype(jnp.bfloat16)
    w_output = output_weight[0]
    summed = lax.psum_scatter(
        jnp.dot(attended, w_output, preferred_element_type=jnp.float32).astype(jnp.bfloat16),
        "dp",
        scatter_dimension=0,
        tiled=True,
    ).astype(jnp.float32)
    check_out = (checked.astype(jnp.float32) + rms_norm(summed, post_gain[0])).astype(jnp.bfloat16)
    return (moved, new_accumulators, check_out[None, :, :])


def solution(mesh):
    placed = (
        P("section", "dp", None),
        P(),
        P("dp", "section", None),
        P(),
        P("section", "dp"),
        P("section", None),
        P("section", None, "dp"),
        P("section", None, "dp"),
        P("section", "dp", None),
        P("section", None),
    )
    return jax.shard_map(
        on_device,
        mesh=mesh,
        in_specs=placed,
        out_specs=(P("section", "dp", None), P("dp", "section", None), P("section", "dp", None)),
        check_vma=False,
    )
```

profile of v0, /device:TPU:2, one launch (start us, length us, event | category | flops | bytes accessed | tf_op | source)
XLA Modules:
  0.0 224.1 jit_solution(8892449664727114092)
XLA Ops:
  7.2 0.8 reshape.111
  9.5 1.9 gather_fusion.2
  11.4 1.2 broadcast_select_fusion.1
  12.6 6.2 %all-to-all-start = ((bf16[8,16,4608]{2,1,0:T(8,128)(2,1)}), bf16[8,16,4608]{2,1,0:T(8,128)(2,1)S(1)}, u32[]{:S(2)}, u32[]{:S(2)}) async-start(bf16[8,16,4608]{2,1,0:T(8,128)(2,1)} %broadcast_select_fusion.1), calls=%async_computation | async-start | bytes 2359296 | tf_op jit(solution)/shard_map/all_to_all | solution.py:83
  19.0 14.8 %all-to-all-done = bf16[8,16,4608]{2,1,0:T(8,128)(2,1)S(1)} async-done(((bf16[8,16,4608]{2,1,0:T(8,128)(2,1)}), bf16[8,16,4608]{2,1,0:T(8,128)(2,1)S(1)}, u32[]{:S(2)}, u32[]{:S(2)}) %all-to-all-start) | async-done | bytes 1179680 | tf_op jit(solution)/shard_map/all_to_all | solution.py:83
  34.6 1.0 copy-done.3
  38.2 61.9 %all-gather.3.cloned.1.call-done = bf16[1,512,4608]{2,1,0:T(8,128)(2,1)} async-done(((bf16[1,16,4608]{2,1,0:T(8,128)(2,1)}), bf16[1,512,4608]{2,1,0:T(8,128)(2,1)}) %all-gather.3.cloned.1.call-update) | async-done | bytes 4718608 | tf_op jit(solution)/shard_map/all_gather | solution.py:113
  100.2 3.5 %fusion = f32[512]{0:T(512)S(1)} fusion(bf16[1,512,4608]{2,1,0:T(8,128)(2,1)} %all-gather.3.cloned.1.call-done), kind=kLoop, calls=%fused_computation.8 | loop fusion | flops 7077376 | bytes 4720640 | tf_op jit(solution)/shard_map/reduce_sum | solution.py:31
  103.9 1.8 fusion.7
  106.9 1.8 fusion.9
  109.7 3.9 %convolution_convert_fusion = bf16[512,4608]{1,0:T(8,128)(2,1)} fusion(bf16[1,128,4608]{2,1,0:T(8,128)(2,1)S(1)} %copy-done, bf16[512,512]{0,1:T(8,128)(2,1)S(1)} %get-tuple-element.28, f32[512]{0:T(512)S(1)} %get-tuple-element.27, bf16[512,128]{0,1:T(8,128)(2,1)S(1)} %collective-permute-done, bf16[512,128]{0,1:T(8,128)(2,1)S(1)} %fusion.21, pred[]{:T(512)S(6)} %eq.57), kind=kOutput, calls=%fused_computation.11 | convolution fusion | flops 673644544 | bytes 6686721 | tf_op jit(solution)/shard_map/dot_general | solution.py:145
  113.7 1.2 copy-done.4
  114.9 1.8 gather_fusion.4
  118.1 2.0 copy.22
  120.1 6.5 %all-to-all-start.1 = ((bf16[32,1,9217]{2,1,0:T(2,128)(2,1)}), bf16[32,1,9217]{2,1,0:T(2,128)(2,1)S(1)}, u32[]{:S(2)}, u32[]{:S(2)}) async-start(bf16[32,1,9217]{2,1,0:T(2,128)(2,1)} %copy.22), calls=%async_computation.1 | async-start | bytes 2392064 | tf_op jit(solution)/shard_map/all_to_all | solution.py:13
  127.5 32.2 %all-to-all-done.1 = bf16[32,1,9217]{2,1,0:T(2,128)(2,1)S(1)} async-done(((bf16[32,1,9217]{2,1,0:T(2,128)(2,1)}), bf16[32,1,9217]{2,1,0:T(2,128)(2,1)S(1)}, u32[]{:S(2)}, u32[]{:S(2)}) %all-to-all-start.1) | async-done | bytes 589920 | tf_op jit(solution)/shard_map/all_to_all | solution.py:13
  159.8 0.8 copy-done.2
  160.7 1.0 reshape.118
  161.7 1.8 gather_fusion.5
  163.5 1.3 convert_reduce_fusion
  165.4 1.6 select_multiply_fusion
  167.1 47.4 %reduce-scatter.2.cloned.1.call-done = bf16[16,4608]{1,0:T(8,128)(2,1)} async-done(((bf16[512,4608]{1,0:T(8,128)(2,1)}), bf16[16,4608]{1,0:T(8,128)(2,1)}) %reduce-scatter.2.cloned.1.call-update) | async-done | bytes 147472 | tf_op jit(solution)/shard_map/reduce_scatter | solution.py:144
  214.4 1.1 fusion.17
  215.5 1.8 fusion.30
  (76 shorter events, 9.1 us)
Async XLA Ops:
  7.2 102.5 %copy-start = (bf16[1,128,4608]{2,1,0:T(8,128)(2,1)S(1)}, bf16[1,128,4608]{2,1,0:T(8,128)(2,1)}, u32[]{:S(2)}) copy-start(bf16[1,128,4608]{2,1,0:T(8,128)(2,1)} %param.22) | copy-start | bytes 3538948
  12.6 21.2 %all-to-all-start = ((bf16[8,16,4608]{2,1,0:T(8,128)(2,1)}), bf16[8,16,4608]{2,1,0:T(8,128)(2,1)S(1)}, u32[]{:S(2)}, u32[]{:S(2)}) async-start(bf16[8,16,4608]{2,1,0:T(8,128)(2,1)} %broadcast_select_fusion.1), calls=%async_computation | async-start | bytes 2359296 | tf_op jit(solution)/shard_map/all_to_all | solution.py:83
  18.7 81.4 %all-gather.3.cloned.1.call-start = ((), (), s32[]{:S(2)}) async-start(), calls=%async_computation.4 | async-start | bytes 4866048 | tf_op jit(solution)/shard_map/all_gather | solution.py:113
  34.4 2.0 copy-start.8
  34.4 2.2 copy-start.6
  34.6 1.0 copy-start.3
  35.6 68.0 %copy-start.9 = (bf16[1,4608,128]{2,1,0:T(8,128)(2,1)S(1)}, bf16[1,4608,128]{2,1,0:T(8,128)(2,1)}, u32[]{:S(2)}) copy-start(bf16[1,4608,128]{2,1,0:T(8,128)(2,1)} %param.21) | copy-start | bytes 3538948
  36.3 178.1 %reduce-scatter.2.cloned.1.call-start = ((), (), s32[]{:S(2)}) async-start(), calls=%async_computation.3 | async-start | bytes 4866048 | tf_op jit(solution)/shard_map/reduce_scatter | solution.py:144
  100.2 3.8 %copy-start.1 = (bf16[1,512,4608]{2,1,0:T(8,128)(2,1)S(1)}, bf16[1,512,4608]{2,1,0:T(8,128)(2,1)}, u32[]{:S(2)}) copy-start(bf16[1,512,4608]{2,1,0:T(8,128)(2,1)} %all-gather.3.cloned.1.call-done) | copy-start | bytes 14155780
  103.9 2.9 %copy-start.10 = (bf16[1,4608,128]{2,1,0:T(8,128)(2,1)S(1)}, bf16[1,4608,128]{2,1,0:T(8,128)(2,1)}, u32[]{:S(2)}) copy-start(bf16[1,4608,128]{2,1,0:T(8,128)(2,1)} %param.20) | copy-start | bytes 3538948
  106.4 2.9 %collective-permute-start = (bf16[512,128]{0,1:T(8,128)(2,1)S(1)}, bf16[512,128]{0,1:T(8,128)(2,1)S(1)}, u32[]{:S(2)}, u32[]{:S(2)}) collective-permute-start(bf16[512,128]{0,1:T(8,128)(2,1)S(1)} %fusion.21), channel_id=1, source_target_pairs={{0,1},{1,0},{2,3},{3,2},{4,5},{5,4},{6,7},{7,6},{8,9},{9,8},{10,11... | collective-permute-start | bytes 393224 | tf_op jit(solution)/shard_map/ppermute | solution.py:27
  113.6 1.3 copy-start.4
  120.1 6.6 %copy-start.7 = (f32[1,4608]{1,0:T(1,128)S(1)}, f32[1,4608]{1,0:T(1,128)}, u32[]{:S(2)}) copy-start(f32[1,4608]{1,0:T(1,128)} %param.23) | copy-start | bytes 55300
  120.1 39.7 %all-to-all-start.1 = ((bf16[32,1,9217]{2,1,0:T(2,128)(2,1)}), bf16[32,1,9217]{2,1,0:T(2,128)(2,1)S(1)}, u32[]{:S(2)}, u32[]{:S(2)}) async-start(bf16[32,1,9217]{2,1,0:T(2,128)(2,1)} %copy.22), calls=%async_computation.1 | async-start | bytes 2392064 | tf_op jit(solution)/shard_map/all_to_all | solution.py:13
  159.8 0.8 copy-start.2
  165.4 50.1 %copy-start.5 = (f32[4608]{0:T(1024)S(1)}, f32[4608]{0:T(1024)}, u32[]{:S(2)}) copy-start(f32[4608]{0:T(1024)} %reduce.2) | copy-start | bytes 55300
Sparse Core Ops, SparseCore 0:
  36.5 63.6 all-gather.2
  113.8 100.6 reduce-scatter.1
where the time goes:
time: 225 us; the launch traced here: 224 us
  waiting for transfers between devices  156 us (69%)
  local copies, waits for them, and re-layouts  15.7 us (7%)
  between operations  15.6 us (7%)
  other arithmetic  15.2 us (7%)
  starting transfers between devices  13.3 us (6%)
  matrix products  8 us (4%)
    all_gather x1, waiting for transfers between devices, on_device(): block_rows = lax.all_gather(checked, 'dp', axis=0, tiled=True)  61.9 us
    reduce_scatter x1, waiting for transfers between devices, on_device(): lax.psum_scatter(jnp.dot(attended, w_output, preferred_element_type=jnp.f...  47.4 us
    all_to_all x1, waiting for transfers between devices, sent_together(): lax.all_to_all(both, axis, split_axis=split_dim, concat_axis=concat_dim,...  32.2 us
    all_to_all x1, waiting for transfers between devices, on_device(): lax.all_to_all(outgoing, 'section', split_axis=0, concat_axis=0, tiled=True)  14.8 us
    all_to_all x1, starting transfers between devices, sent_together(): lax.all_to_all(both, axis, split_axis=split_dim, concat_axis=concat_dim,...  6.54 us
    all_to_all x1, starting transfers between devices, on_device(): lax.all_to_all(outgoing, 'section', split_axis=0, concat_axis=0, tiled=True)  6.18 us
    reduce_sum x2, other arithmetic, rms_norm(): meansq = jnp.mean(values * values, axis=-1, keepdims=True)  4.54 us
  transfers between devices with their start and end apart: 5, of which 4 were waited for; matrix products, arithmetic and copies ran while one was open for 7% of the time, Pallas kernels for 0%

commit v1 on v0

--- a/solution.py
+++ b/solution.py
@@ -110,7 +110,9 @@
     w_query = query_weight[0]
     w_keyval = keyval_weight[0]
     gain_pre = pre_gain[0]
-    block_rows = lax.all_gather(checked, "dp", axis=0, tiled=True)
+    block_rows = jnp.concatenate(
+        lax.all_to_all(jnp.stack([checked] * lax.axis_size("dp")), "dp", 0, 0), axis=0
+    )
     row_count = block_rows.shape[0]
     positions = jnp.arange(row_count, dtype=jnp.int32)
     normed = rms_norm(block_rows.astype(jnp.float32), gain_pre).astype(jnp.bfloat16)

time: 225 us -> 285 us (1.27)
  waiting for transfers between devices: 156 us -> 189 us
  starting transfers between devices: 13.3 us -> 36 us
  other arithmetic: 15.2 us -> 19 us
    all_to_all x0 -> x1, waiting for transfers between devices: none -> 83.5 us  [on_device(): lax.all_to_all(jnp.stack([checked] * lax.axis_size('dp')), 'dp', 0, 0)]
    all_gather x1 -> x0, waiting for transfers between devices: 61.9 us -> none  [on_device(): block_rows = lax.all_gather(checked, 'dp', axis=0, tiled=True)]
    reduce_scatter x1, waiting for transfers between devices: 47.4 us -> 63.9 us  [on_device(): lax.psum_scatter(jnp.dot(attended, w_output, preferred_element_type=jnp.f...]
    all_to_all x1, starting transfers between devices: 6.54 us -> 18.6 us  [sent_together(): lax.all_to_all(both, axis, split_axis=split_dim, concat_axis=concat_dim,...]
    all_to_all x0 -> x1, starting transfers between devices: none -> 10.8 us  [on_device(): lax.all_to_all(jnp.stack([checked] * lax.axis_size('dp')), 'dp', 0, 0)]
    all_to_all x1, waiting for transfers between devices: 32.2 us -> 26.3 us  [sent_together(): lax.all_to_all(both, axis, split_axis=split_dim, concat_axis=concat_dim,...]
    convert_element_type x0 -> x1, other arithmetic: none -> 3.98 us  [on_device(): rms_norm(block_rows.astype(jnp.float32), gain_pre).astype(jnp.bfloat16)]
  transfers between devices with their start and end apart: 5 -> 5, of which waited for: 4 -> 4; matrix products, arithmetic and copies ran while one was open for 7% -> 5% of each run, Pallas kernels for 0% -> 0%
where the time goes in v1:
time: 285 us; the launch traced here: 284 us
  waiting for transfers between devices  189 us (66%)
  starting transfers between devices  36 us (13%)
  other arithmetic  19 us (7%)
  local copies, waits for them, and re-layouts  17.5 us (6%)
  between operations  15.6 us (5%)
  matrix products  7.71 us (3%)
    all_to_all x1, waiting for transfers between devices, on_device(): lax.all_to_all(jnp.stack([checked] * lax.axis_size('dp')), 'dp', 0, 0)  83.5 us
    reduce_scatter x1, waiting for transfers between devices, on_device(): lax.psum_scatter(jnp.dot(attended, w_output, preferred_element_type=jnp.f...  63.9 us
    all_to_all x1, waiting for transfers between devices, sent_together(): lax.all_to_all(both, axis, split_axis=split_dim, concat_axis=concat_dim,...  26.3 us
    all_to_all x1, starting transfers between devices, sent_together(): lax.all_to_all(both, axis, split_axis=split_dim, concat_axis=concat_dim,...  18.6 us
    all_to_all x1, waiting for transfers between devices, on_device(): lax.all_to_all(outgoing, 'section', split_axis=0, concat_axis=0, tiled=True)  14.8 us
    all_to_all x1, starting transfers between devices, on_device(): lax.all_to_all(jnp.stack([checked] * lax.axis_size('dp')), 'dp', 0, 0)  10.8 us
    all_to_all x1, starting transfers between devices, on_device(): lax.all_to_all(outgoing, 'section', split_axis=0, concat_axis=0, tiled=True)  6.18 us
  transfers between devices with their start and end apart: 5, of which 4 were waited for; matrix products, arithmetic and copies ran while one was open for 5% of the time, Pallas kernels for 0%

profile of v1, /device:TPU:2, one launch (start us, length us, event | category | flops | bytes accessed | tf_op | source)
XLA Modules:
  0.0 284.3 jit_solution(4654186658810611886)
XLA Ops:
  9.5 1.9 gather_fusion.2
  11.4 1.2 broadcast_select_fusion.1
  12.6 6.2 %all-to-all-start = ((bf16[8,16,4608]{2,1,0:T(8,128)(2,1)}), bf16[8,16,4608]{2,1,0:T(8,128)(2,1)S(1)}, u32[]{:S(2)}, u32[]{:S(2)}) async-start(bf16[8,16,4608]{2,1,0:T(8,128)(2,1)} %broadcast_select_fusion.1), calls=%async_computation | async-start | bytes 2359296 | tf_op jit(solution)/shard_map/all_to_all | solution.py:83
  19.0 14.8 %all-to-all-done = bf16[8,16,4608]{2,1,0:T(8,128)(2,1)S(1)} async-done(((bf16[8,16,4608]{2,1,0:T(8,128)(2,1)}), bf16[8,16,4608]{2,1,0:T(8,128)(2,1)S(1)}, u32[]{:S(2)}, u32[]{:S(2)}) %all-to-all-start) | async-done | bytes 1179680 | tf_op jit(solution)/shard_map/all_to_all | solution.py:83
  34.6 1.0 copy-done.2
  35.6 2.7 stack.3
  38.3 10.8 %all-to-all-start.2 = ((bf16[32,16,4608]{2,1,0:T(8,128)(2,1)}), bf16[32,16,4608]{2,1,0:T(8,128)(2,1)}, u32[]{:S(2)}, u32[]{:S(2)}) async-start(bf16[32,16,4608]{2,1,0:T(8,128)(2,1)} %stack.3), calls=%async_computation.2 | async-start | bytes 9437184 | tf_op jit(solution)/shard_map/all_to_all | solution.py:114
  51.1 83.5 %all-to-all-done.2 = bf16[32,16,4608]{2,1,0:T(8,128)(2,1)} async-done(((bf16[32,16,4608]{2,1,0:T(8,128)(2,1)}), bf16[32,16,4608]{2,1,0:T(8,128)(2,1)}, u32[]{:S(2)}, u32[]{:S(2)}) %all-to-all-start.2) | async-done | bytes 4718624 | tf_op jit(solution)/shard_map/all_to_all | solution.py:114
  134.5 3.3 %fusion = f32[32,16]{1,0:T(8,128)S(1)} fusion(bf16[32,16,4608]{2,1,0:T(8,128)(2,1)} %all-to-all-done.2), kind=kLoop, calls=%fused_computation.8 | loop fusion | flops 7077376 | bytes 4720640 | tf_op jit(solution)/shard_map/reduce_sum | solution.py:31
  137.9 4.0 %fusion.2 = bf16[32,16,4608]{2,1,0:T(8,128)(2,1)S(1)} fusion(bf16[32,16,4608]{2,1,0:T(8,128)(2,1)} %all-to-all-done.2, f32[4608]{0:T(1024)S(1)} %reduce.2, f32[32,16]{1,0:T(8,128)S(1)} %add_rsqrt_fusion), kind=kLoop, calls=%fused_computation.10 | loop fusion | flops 9437184 | bytes 9457664 | tf_op jit(solution)/shard_map/convert_element_type | solution.py:118
  141.9 1.7 fusion.8
  144.5 1.7 fusion.10
  147.2 3.9 %convolution_convert_fusion = bf16[512,4608]{1,0:T(8,128)(2,1)} fusion(bf16[1,128,4608]{2,1,0:T(8,128)(2,1)S(1)} %copy-done, bf16[512,512]{0,1:T(8,128)(2,1)S(1)} %get-tuple-element.28, f32[512]{0:T(512)S(1)} %get-tuple-element.27, bf16[512,128]{0,1:T(8,128)(2,1)S(1)} %collective-permute-done, bf16[512,128]{0,1:T(8,128)(2,1)S(1)} %fusion.19, pred[]{:T(512)S(6)} %eq.57), kind=kOutput, calls=%fused_computation.11 | convolution fusion | flops 673644544 | bytes 6686721 | tf_op jit(solution)/shard_map/dot_general | solution.py:147
  151.2 1.2 copy-done.5
  152.4 1.8 gather_fusion.4
  155.6 2.0 copy.22
  157.5 18.6 %all-to-all-start.1 = ((bf16[32,1,9217]{2,1,0:T(2,128)(2,1)}), bf16[32,1,9217]{2,1,0:T(2,128)(2,1)S(1)}, u32[]{:S(2)}, u32[]{:S(2)}) async-start(bf16[32,1,9217]{2,1,0:T(2,128)(2,1)} %copy.22), calls=%async_computation.1 | async-start | bytes 2392064 | tf_op jit(solution)/shard_map/all_to_all | solution.py:13
  177.1 26.3 %all-to-all-done.1 = bf16[32,1,9217]{2,1,0:T(2,128)(2,1)S(1)} async-done(((bf16[32,1,9217]{2,1,0:T(2,128)(2,1)}), bf16[32,1,9217]{2,1,0:T(2,128)(2,1)S(1)}, u32[]{:S(2)}, u32[]{:S(2)}) %all-to-all-start.1) | async-done | bytes 589920 | tf_op jit(solution)/shard_map/all_to_all | solution.py:13
  205.4 1.8 gather_fusion.5
  207.2 1.3 convert_reduce_fusion
  209.1 1.6 select_multiply_fusion
  210.7 63.9 %reduce-scatter.2.cloned.1.call-done = bf16[16,4608]{1,0:T(8,128)(2,1)} async-done(((bf16[512,4608]{1,0:T(8,128)(2,1)}), bf16[16,4608]{1,0:T(8,128)(2,1)}) %reduce-scatter.2.cloned.1.call-update) | async-done | bytes 147472 | tf_op jit(solution)/shard_map/reduce_scatter | solution.py:146
  274.6 1.1 fusion.15
  275.7 1.8 fusion.28
  (75 shorter events, 10.6 us)
Async XLA Ops:
  7.2 140.0 %copy-start = (bf16[1,128,4608]{2,1,0:T(8,128)(2,1)S(1)}, bf16[1,128,4608]{2,1,0:T(8,128)(2,1)}, u32[]{:S(2)}) copy-start(bf16[1,128,4608]{2,1,0:T(8,128)(2,1)} %param.22) | copy-start | bytes 3538948
  12.6 21.2 %all-to-all-start = ((bf16[8,16,4608]{2,1,0:T(8,128)(2,1)}), bf16[8,16,4608]{2,1,0:T(8,128)(2,1)S(1)}, u32[]{:S(2)}, u32[]{:S(2)}) async-start(bf16[8,16,4608]{2,1,0:T(8,128)(2,1)} %broadcast_select_fusion.1), calls=%async_computation | async-start | bytes 2359296 | tf_op jit(solution)/shard_map/all_to_all | solution.py:83
  34.6 1.0 copy-start.2
  38.3 10.9 %copy-start.9 = (s32[1024]{0:T(1024)S(1)}, s32[1024]{0:T(1024)}, u32[]{:S(2)}) copy-start(s32[1024]{0:T(1024)} %param.17) | copy-start | bytes 12292
  38.3 11.1 %copy-start.7 = (f32[1,4608]{1,0:T(1,128)S(1)}, f32[1,4608]{1,0:T(1,128)}, u32[]{:S(2)}) copy-start(f32[1,4608]{1,0:T(1,128)} %param.19) | copy-start | bytes 55300
  38.3 96.2 %all-to-all-start.2 = ((bf16[32,16,4608]{2,1,0:T(8,128)(2,1)}), bf16[32,16,4608]{2,1,0:T(8,128)(2,1)}, u32[]{:S(2)}, u32[]{:S(2)}) async-start(bf16[32,16,4608]{2,1,0:T(8,128)(2,1)} %stack.3), calls=%async_computation.2 | async-start | bytes 9437184 | tf_op jit(solution)/shard_map/all_to_all | solution.py:114
  49.2 225.4 %reduce-scatter.2.cloned.1.call-start = ((), (), s32[]{:S(2)}) async-start(), calls=%async_computation.4 | async-start | bytes 4866048 | tf_op jit(solution)/shard_map/reduce_scatter | solution.py:146
  137.9 4.0 %copy-start.3 = (bf16[1,4608,128]{2,1,0:T(8,128)(2,1)S(1)}, bf16[1,4608,128]{2,1,0:T(8,128)(2,1)}, u32[]{:S(2)}) copy-start(bf16[1,4608,128]{2,1,0:T(8,128)(2,1)} %param.21) | copy-start | bytes 3538948
  141.9 2.6 copy-start.4
  144.2 2.6 collective-permute-start
  151.1 1.3 copy-start.5
  157.5 18.7 %copy-start.8 = (f32[1,4608]{1,0:T(1,128)S(1)}, f32[1,4608]{1,0:T(1,128)}, u32[]{:S(2)}) copy-start(f32[1,4608]{1,0:T(1,128)} %param.23) | copy-start | bytes 55300
  157.5 45.9 %all-to-all-start.1 = ((bf16[32,1,9217]{2,1,0:T(2,128)(2,1)}), bf16[32,1,9217]{2,1,0:T(2,128)(2,1)S(1)}, u32[]{:S(2)}, u32[]{:S(2)}) async-start(bf16[32,1,9217]{2,1,0:T(2,128)(2,1)} %copy.22), calls=%async_computation.1 | async-start | bytes 2392064 | tf_op jit(solution)/shard_map/all_to_all | solution.py:13
  203.5 0.8 copy-start.1
  209.1 66.6 %copy-start.6 = (f32[4608]{0:T(1024)S(1)}, f32[4608]{0:T(1024)}, u32[]{:S(2)}) copy-start(f32[4608]{0:T(1024)} %reduce.3) | copy-start | bytes 55300
Sparse Core Ops, SparseCore 0:
  151.2 123.3 reduce-scatter.1
